TPU v7x, 128 devices: a whole 4x4x4 slice. The times are simulated.
128 devices in a mesh: rows: 16 (over z, x), cols: 8 (over y, core).
Axes of the slice: x: 4, y: 4, z: 4, core: 2. Of those that a mesh axis runs over, the one named last changes fastest.
Arguments:
- densities: bfloat16 [6, 8192, 128, 128], P(None, ('rows', 'cols')), may hold values from -6 to 6
- residuals: bfloat16 [6, 8192, 128, 128], P(None, ('rows', 'cols')), may hold values from -32 to 32
- block_pairs: int32 [2, 8192], P(None, ('rows', 'cols')), may hold values from 0 to 1562
- new_owner: int32 [8192], P(('rows', 'cols')), may hold values from -1 to 15, as said below
Outputs:
- owned_blocks: bfloat16 [4096, 128, 128], P(('rows', 'cols'))
- coefficients: float32 [6], replicated
Inputs may be any that keep to these rules, and one draw needn't show every extreme that they name: A live block stays at its index of cols and moves to index new_owner of rows. For each index of cols, every index of rows becomes the owner of exactly 32 blocks, and at most 4 of them come from one device.
All inputs are finite; a program needn't handle non-finite values.
Results may differ from a plain program's by a relative error of at most 0.0019.
Values may be sent and summed in bfloat16 or wider, within the bound.
A program may use at most 128 MiB of HBM per device.

v0:
```python
import math
import jax
import jax.numpy as jnp
from jax import lax
from jax.sharding import Mesh
from jax.sharding import PartitionSpec as P

OWNED = 32
ROWS = ("rows_0", "rows_1")
ROWS_COLS = ("rows_0", "rows_1", "cols_0", "cols_1")
mix_weight = 0.3


def over_axes(shard, axes):
    for axis in axes:
        shard = lax.psum(shard, axis)
    return shard


def sent_together(arrays, axis, split_dim, concat_dim, along):
    widths = [math.prod(a.shape[along:]) for a in arrays]
    both = jnp.concatenate(
        [a.reshape(*a.shape[:along], w) for a, w in zip(arrays, widths)], axis=along
    )
    whole = lax.all_to_all(both, axis, split_axis=split_dim, concat_axis=concat_dim, tiled=True)
    pieces = jnp.split(whole, [sum(widths[:k]) for k in range(1, len(widths))], axis=along)
    return tuple(
        (b.reshape(*whole.shape[:along], *a.shape[along:]) for a, b in zip(arrays, pieces))
    )


def small_solve(system, vector):
    order_n = system.shape[0]
    positions = jnp.arange(order_n, dtype=jnp.int32)
    for step_index in range(order_n):
        column = system[:, step_index] / system[step_index, step_index]
        column = jnp.where(positions > step_index, column, 0.0)
        system = system - column[:, None] * system[step_index][None, :]
        vector = vector - column * vector[step_index]
    solution = jnp.zeros((order_n,), jnp.float32)
    for step_index in reversed(range(order_n)):
        inner = jnp.sum(jnp.where(positions > step_index, system[step_index] * solution, 0.0))
        solution = solution.at[step_index].set(
            (vector[step_index] - inner) / system[step_index, step_index]
        )
    return solution


def slot_correlation(residual_set, weights):
    flattened = residual_set.reshape(residual_set.shape[0], residual_set.shape[1], -1)
    per_slot = jnp.einsum("isn,ksn->sik", flattened, flattened, preferred_element_type=jnp.float32)
    return jnp.einsum("s,sik->ik", weights, per_slot)


def blend_history(density_set, residual_set, coefficients):
    running = jnp.zeros(density_set.shape[1:], jnp.float32)
    for hist_index in range(density_set.shape[0]):
        running = running + coefficients[hist_index] * (
            density_set[hist_index].astype(jnp.float32)
            + mix_weight * residual_set[hist_index].astype(jnp.float32)
        )
    return running.astype(jnp.bfloat16)


def compact_order(arrived_weights):
    usable = arrived_weights > 0.0
    position = jnp.cumsum(usable.astype(jnp.int32)) - 1
    spots = jnp.where(usable, position, OWNED)
    count_in = arrived_weights.shape[0]
    return (
        jnp.zeros((OWNED,), jnp.int32)
        .at[spots]
        .set(jnp.arange(count_in, dtype=jnp.int32), mode="drop")
    )


def on_device(densities, residuals, block_pairs, new_owner):
    rows_count = lax.axis_size(ROWS)
    held_slots = new_owner.shape[0]
    pair_cap = 2 * OWNED // rows_count
    sent_count = rows_count * pair_cap
    alive_slot = new_owner >= 0
    weights = jnp.where(
        alive_slot, jnp.where(block_pairs[0] == block_pairs[1], 1.0, 2.0), 0.0
    ).astype(jnp.float32)
    owner_rows = jnp.where(alive_slot, new_owner, rows_count)
    onehot = (owner_rows[:, None] == jnp.arange(rows_count, dtype=jnp.int32)[None, :]).astype(
        jnp.int32
    )
    ranking = jnp.sum(jnp.cumsum(onehot, axis=0) * onehot, axis=1) - 1
    placing = jnp.where(alive_slot, owner_rows * pair_cap + ranking, sent_count)
    slot_table = (
        jnp.full((sent_count,), held_slots, jnp.int32)
        .at[placing]
        .set(jnp.arange(held_slots, dtype=jnp.int32), mode="drop")
    )
    chosen = jnp.minimum(slot_table, held_slots - 1)
    sent_weights = jnp.where(slot_table < held_slots, weights[chosen], 0.0).astype(jnp.bfloat16)
    partial_correlation = slot_correlation(residuals, weights)
    correlation = over_axes(partial_correlation, ROWS_COLS)
    solved = small_solve(correlation, jnp.ones((correlation.shape[0],), jnp.float32))
    coefficients = solved / jnp.sum(solved)
    mixed_blocks = blend_history(densities, residuals, coefficients)
    arrived = sent_together((jnp.take(mixed_blocks, chosen, axis=0), sent_weights), ROWS, 0, 0, 1)
    ordering = compact_order(arrived[1].astype(jnp.float32))
    owned_blocks = jnp.take(arrived[0], ordering, axis=0)
    return (owned_blocks, coefficients)


def solution(mesh):
    finer = Mesh(mesh.devices.reshape(4, 4, 4, 2), ("rows_0", "rows_1", "cols_0", "cols_1"))
    placed = (
        P(None, ROWS_COLS, None, None),
        P(None, ROWS_COLS, None, None),
        P(None, ROWS_COLS),
        P(ROWS_COLS),
    )
    return jax.shard_map(
        on_device,
        mesh=finer,
        in_specs=placed,
        out_specs=(P(ROWS_COLS, None, None), P()),
        check_vma=False,
    )
```

profile of v0, /device:TPU:0, one launch (start us, length us, event | category | flops | bytes accessed | tf_op | source)
XLA Modules:
  0.0 182.0 jit_solution(14039004211042699980)
XLA Ops:
  0.6 19.3 %reshape.282 = bf16[6,64,16384]{2,1,0:T(8,128)(2,1)} reshape(bf16[6,64,128,128]{3,2,1,0:T(8,128)(2,1)} %param.17) | data formatting | bytes 25165824 | tf_op jit(solution)/shard_map/reshape | solution.py:50
  20.0 25.8 %fusion = bf16[64,6,6]{2,1,0:T(8,128)(2,1)S(1)} fusion(bf16[6,64,16384]{2,1,0:T(8,128)(2,1)} %reshape.282), kind=kOutput, calls=%fused_computation.5 | convolution fusion | flops 75497472 | bytes 12587520 | tf_op jit(solution)/shard_map/isn,ksn->sik/dot_general | solution.py:51
  45.9 11.9 %psum.28 = f32[6,6]{1,0:T(8,128)S(1)} all-reduce(f32[6,6]{1,0:T(8,128)S(1)} %bitcast.87), channel_id=1, replica_groups=mesh['rows_0'=4,'rows_1'=4,'cols_0'=4,'cols_1'=2] {'rows_0'}, use_global_device_ids=true, to_apply=%region_3.4 | all-reduce | flops 36 | bytes 288 | tf_op jit(solution)/shard_map/psum | solution.py:16
  57.8 10.5 %psum.29 = f32[6,6]{1,0:T(8,128)S(1)} all-reduce(f32[6,6]{1,0:T(8,128)S(1)} %psum.28), channel_id=1, replica_groups=mesh['rows_0'=4,'rows_1'=4,'cols_0'=4,'cols_1'=2] {'rows_1'}, use_global_device_ids=true, to_apply=%region_4.5 | all-reduce | flops 36 | bytes 288 | tf_op jit(solution)/shard_map/psum | solution.py:16
  68.3 10.7 %psum.30 = f32[6,6]{1,0:T(8,128)S(1)} all-reduce(f32[6,6]{1,0:T(8,128)S(1)} %psum.29), channel_id=1, replica_groups=mesh['rows_0'=4,'rows_1'=4,'cols_0'=4,'cols_1'=2] {'cols_0'}, use_global_device_ids=true, to_apply=%region_5.6 | all-reduce | flops 36 | bytes 288 | tf_op jit(solution)/shard_map/psum | solution.py:16
  79.0 2.5 %psum.31 = f32[6,6]{1,0:T(8,128)S(1)} all-reduce(f32[6,6]{1,0:T(8,128)S(1)} %psum.30), channel_id=1, replica_groups=mesh['rows_0'=4,'rows_1'=4,'cols_0'=4,'cols_1'=2] {'cols_1'}, use_global_device_ids=true, to_apply=%region_6.7 | all-reduce | flops 36 | bytes 288 | tf_op jit(solution)/shard_map/psum | solution.py:16
  82.0 0.8 fusion.7
  82.8 0.6 slice.248
  83.4 0.8 select_reduce_fusion.5
  84.4 0.6 slice.252
  84.9 0.8 select_reduce_fusion.4
  85.8 0.6 slice.256
  86.4 0.8 select_reduce_fusion.3
  87.3 0.6 slice.260
  87.9 0.8 select_reduce_fusion.2
  88.8 0.6 slice.264
  89.4 0.8 select_reduce_fusion.1
  90.3 0.7 fusion.38
  91.0 0.7 fusion.30
  91.7 0.6 slice.249
  92.3 0.6 fusion.17
  93.5 0.6 fusion.20
  94.7 0.6 fusion.23
  96.0 0.6 fusion.26
  97.2 0.6 fusion.29
  97.9 0.7 fusion.40
  100.6 0.8 fusion.27
  103.3 0.6 fusion.24
  105.8 0.7 fusion.21
  108.4 0.6 fusion.18
  111.0 0.6 fusion.15
  113.6 0.6 reduce_sum.79
  114.2 0.6 broadcast_divide_fusion
  114.9 0.7 fusion.39
  115.9 1.0 scatter_custom_fusion
  116.9 0.8 gather_fusion.1
  117.7 15.0 %fusion.2 = bf16[64,128,128]{2,1,0:T(8,128)(2,1)S(1)} fusion(bf16[6,64,128,128]{3,2,1,0:T(8,128)(2,1)} %param.17, bf16[6,64,128,128]{3,2,1,0:T(8,128)(2,1)} %param.16, f32[]{:T(128)} %bitcast.49, f32[]{:T(128)} %bitcast.48, f32[]{:T(128)} %bitcast.47, f32[]{:T(128)} %bitcast.46, f32[]{:T(128)} %bitcast.45, f32[]{:T(128)} %bitcast.44), kind=kLoop, calls=%fused_computation.11 | loop fusion | flops 37748736 | bytes 27263000 | tf_op jit(solution)/shard_map/convert_element_type | solution.py:62
  132.7 2.2 %gather_fusion = bf16[64,128,128]{2,1,0:T(8,128)(2,1)} fusion(bf16[64,128,128]{2,1,0:T(8,128)(2,1)S(1)} %fusion.2, s32[1024]{0:T(1024)S(1)} %pad_clamp_fusion.1), kind=kCustom, calls=%fused_computation | custom fusion | bytes 4194560 | tf_op jit(solution)/shard_map/jit(_take)/gather | solution.py:104
  134.9 2.6 %gather.14 = bf16[16,4,16384]{2,1,0:T(4,128)(2,1)S(1)} reshape(bf16[64,128,128]{2,1,0:T(8,128)(2,1)} %gather_fusion) | data formatting | bytes 4194304 | tf_op jit(solution)/shard_map/jit(_take)/gather | solution.py:104
  137.8 1.0 broadcast_select_fusion
  138.8 1.0 pad_maximum_fusion
  139.7 32.8 %all_to_all.9 = bf16[16,4,16385]{2,1,0:T(4,128)(2,1)} all-to-all(bf16[16,4,16385]{2,1,0:T(4,128)(2,1)S(1)} %pad_maximum_fusion), channel_id=1, replica_groups=mesh['rows_0'=4,'rows_1'=4,'cols_0'=4,'cols_1'=2] {'rows_0','rows_1'}, dimensions={0} | all-to-all | bytes 4194560 | tf_op jit(solution)/shard_map/all_to_all | solution.py:25
  172.5 2.8 %all_to_all.7 = bf16[64,16385]{1,0:T(8,128)(2,1)S(1)} reshape(bf16[16,4,16385]{2,1,0:T(4,128)(2,1)} %all_to_all.9) | data formatting | bytes 4194560 | tf_op jit(solution)/shard_map/all_to_all | solution.py:25
  175.4 1.5 slice_bitcast_fusion
  177.1 0.8 scatter_custom_fusion.1
  177.9 2.2 %copy.11 = bf16[8,8,128,128]{3,2,1,0:T(8,128)(2,1)S(1)} copy(bf16[8,8,128,128]{3,1,2,0:T(8,128)(2,1)} %slice_bitcast_fusion) | data formatting | bytes 4194304
  180.1 0.8 gather_fusion.2
  180.8 1.1 broadcast_select_fusion.1
  (51 shorter events, 4.5 us)
Async XLA Ops:
  20.0 25.8 %copy-start.1 = (s32[2,64]{1,0:T(2,128)S(1)}, s32[2,64]{1,0:T(2,128)}, u32[]{:S(2)}) copy-start(s32[2,64]{1,0:T(2,128)} %param.18) | copy-start | bytes 1540
  20.0 25.8 %copy-start.2 = (s32[64]{0:T(128)S(1)}, s32[64]{0:T(128)}, u32[]{:S(2)}) copy-start(s32[64]{0:T(128)} %param.19) | copy-start | bytes 772
  114.9 17.8 %copy-start = (f32[6]{0:T(128)}, f32[6]{0:T(128)S(1)}, u32[]{:S(2)}) copy-start(f32[6]{0:T(128)S(1)} %broadcast_divide_fusion) | copy-start | bytes 76
where the time goes:
time: 183 us; the launch traced here: 182 us
  blocking collectives  68.4 us (37%)
  local copies, waits for them, and re-layouts  42.7 us (23%)
  other arithmetic  32.5 us (18%)
  matrix products  25.9 us (14%)
  between operations  12.5 us (7%)
    psum x4, blocking collectives, over_axes(): shard = lax.psum(shard, axis)  35.5 us
    all_to_all x1, blocking collectives, sent_together(): lax.all_to_all(both, axis, split_axis=split_dim, concat_axis=concat_dim,...  32.8 us
    dot_general x1, matrix products, slot_correlation(): jnp.einsum('isn,ksn->sik', flattened, flattened, preferred_element_type=j...  25.8 us
    reshape x1, local copies, waits for them, and re-layouts, slot_correlation(): residual_set.reshape(residual_set.shape[0], residual_set.shape[1], -1)  19.3 us
    convert_element_type x1, other arithmetic, blend_history(): return running.astype(jnp.bfloat16)  15 us
    gather x2, local copies, waits for them, and re-layouts, on_device(): jnp.take(mixed_blocks, chosen, axis=0)  4.79 us
    select_n x5, other arithmetic, small_solve(): column = jnp.where(positions > step_index, column, 0.0)  4.13 us
    reduce_sum x6, other arithmetic, small_solve(): jnp.sum(jnp.where(positions > step_index, system[step_index] * solution,...  3.92 us

commit v1 on v0

--- a/solution.py
+++ b/solution.py
@@ -13,7 +13,7 @@
 
 def over_axes(shard, axes):
     for axis in axes:
-        shard = lax.psum(shard, axis)
+        shard = jnp.sum(lax.all_gather(shard, axis), axis=0)
     return shard
 
 

time: 183 us -> 190 us (1.038)
  blocking collectives: 68.4 us -> 75.1 us
    all_gather x0 -> x4, blocking collectives: none -> 40 us  [over_axes(): shard = jnp.sum(lax.all_gather(shard, axis), axis=0)]
    psum x4 -> x0, blocking collectives: 35.5 us -> none  [over_axes(): shard = lax.psum(shard, axis)]
    all_to_all x1, blocking collectives: 32.8 us -> 35 us  [sent_together(): lax.all_to_all(both, axis, split_axis=split_dim, concat_axis=concat_dim,...]
where the time goes in v1:
time: 190 us; the launch traced here: 189 us
  blocking collectives  75.1 us (40%)
  local copies, waits for them, and re-layouts  42.7 us (22%)
  other arithmetic  32.5 us (17%)
  matrix products  25.9 us (14%)
  between operations  12.5 us (7%)
    all_gather x4, blocking collectives, over_axes(): shard = jnp.sum(lax.all_gather(shard, axis), axis=0)  40 us
    all_to_all x1, blocking collectives, sent_together(): lax.all_to_all(both, axis, split_axis=split_dim, concat_axis=concat_dim,...  35 us
    dot_general x1, matrix products, slot_correlation(): jnp.einsum('isn,ksn->sik', flattened, flattened, preferred_element_type=j...  25.8 us
    reshape x1, local copies, waits for them, and re-layouts, slot_correlation(): residual_set.reshape(residual_set.shape[0], residual_set.shape[1], -1)  19.3 us
    convert_element_type x1, other arithmetic, blend_history(): return running.astype(jnp.bfloat16)  15 us
    gather x2, local copies, waits for them, and re-layouts, on_device(): jnp.take(mixed_blocks, chosen, axis=0)  4.79 us
    select_n x5, other arithmetic, small_solve(): column = jnp.where(positions > step_index, column, 0.0)  4.13 us
    reduce_sum x6, other arithmetic, small_solve(): jnp.sum(jnp.where(positions > step_index, system[step_index] * solution,...  3.92 us

profile of v1, /device:TPU:0, one launch (start us, length us, event | category | flops | bytes accessed | tf_op | source)
XLA Modules:
  0.0 188.7 jit_solution(14205851705961004455)
XLA Ops:
  0.6 19.3 %reshape.282 = bf16[6,64,16384]{2,1,0:T(8,128)(2,1)} reshape(bf16[6,64,128,128]{3,2,1,0:T(8,128)(2,1)} %param.17) | data formatting | bytes 25165824 | tf_op jit(solution)/shard_map/reshape | solution.py:50
  20.0 25.8 %fusion = bf16[64,6,6]{2,1,0:T(8,128)(2,1)S(1)} fusion(bf16[6,64,16384]{2,1,0:T(8,128)(2,1)} %reshape.282), kind=kOutput, calls=%fused_computation.5 | convolution fusion | flops 75497472 | bytes 12587520 | tf_op jit(solution)/shard_map/isn,ksn->sik/dot_general | solution.py:51
  45.9 13.3 %all-gather.4 = f32[4,6,6]{2,1,0:T(8,128)S(1)} all-gather(f32[1,6,6]{2,1,0:T(8,128)S(1)} %copy.12), channel_id=2, replica_groups=mesh['rows_0'=4,'rows_1'=4,'cols_0'=4,'cols_1'=2] {'rows_0'}, dimensions={0}, use_global_device_ids=true | all-gather | bytes 720 | tf_op jit(solution)/shard_map/all_gather | solution.py:16
  59.2 12.4 %all-gather.5 = f32[4,6,6]{2,1,0:T(8,128)S(1)} all-gather(f32[1,6,6]{2,1,0:T(8,128)S(1)} %bitcast.88), channel_id=3, replica_groups=mesh['rows_0'=4,'rows_1'=4,'cols_0'=4,'cols_1'=2] {'rows_1'}, dimensions={0}, use_global_device_ids=true | all-gather | bytes 720 | tf_op jit(solution)/shard_map/all_gather | solution.py:16
  71.6 12.5 %all-gather.6 = f32[4,6,6]{2,1,0:T(8,128)S(1)} all-gather(f32[1,6,6]{2,1,0:T(8,128)S(1)} %bitcast.89), channel_id=4, replica_groups=mesh['rows_0'=4,'rows_1'=4,'cols_0'=4,'cols_1'=2] {'cols_0'}, dimensions={0}, use_global_device_ids=true | all-gather | bytes 720 | tf_op jit(solution)/shard_map/all_gather | solution.py:16
  84.2 1.8 all-gather.7
  86.5 0.8 fusion.7
  87.4 0.6 slice.248
  88.0 0.8 select_reduce_fusion.5
  88.9 0.6 slice.252
  89.5 0.8 select_reduce_fusion.4
  90.4 0.6 slice.256
  91.0 0.8 select_reduce_fusion.3
  91.9 0.6 slice.260
  92.5 0.8 select_reduce_fusion.2
  93.4 0.6 slice.264
  94.0 0.8 select_reduce_fusion.1
  94.9 0.7 fusion.38
  95.6 0.7 fusion.30
  96.2 0.6 slice.249
  96.8 0.6 fusion.17
  98.0 0.6 fusion.20
  99.3 0.6 fusion.23
  100.5 0.6 fusion.26
  101.8 0.6 fusion.29
  102.4 0.7 fusion.40
  105.1 0.8 fusion.27
  107.9 0.6 fusion.24
  110.4 0.7 fusion.21
  113.0 0.6 fusion.18
  115.5 0.6 fusion.15
  118.1 0.6 reduce_sum.119
  118.7 0.6 broadcast_divide_fusion
  119.4 0.7 fusion.39
  120.5 1.0 scatter_custom_fusion
  121.4 0.8 gather_fusion.1
  122.2 15.0 %fusion.2 = bf16[64,128,128]{2,1,0:T(8,128)(2,1)S(1)} fusion(bf16[6,64,128,128]{3,2,1,0:T(8,128)(2,1)} %param.17, bf16[6,64,128,128]{3,2,1,0:T(8,128)(2,1)} %param.16, f32[]{:T(128)} %bitcast.52, f32[]{:T(128)} %bitcast.51, f32[]{:T(128)} %bitcast.50, f32[]{:T(128)} %bitcast.49, f32[]{:T(128)} %bitcast.48, f32[]{:T(128)} %bitcast.47), kind=kLoop, calls=%fused_computation.11 | loop fusion | flops 37748736 | bytes 27263000 | tf_op jit(solution)/shard_map/convert_element_type | solution.py:62
  137.2 2.2 %gather_fusion = bf16[64,128,128]{2,1,0:T(8,128)(2,1)} fusion(bf16[64,128,128]{2,1,0:T(8,128)(2,1)S(1)} %fusion.2, s32[1024]{0:T(1024)S(1)} %pad_clamp_fusion.1), kind=kCustom, calls=%fused_computation | custom fusion | bytes 4194560 | tf_op jit(solution)/shard_map/jit(_take)/gather | solution.py:104
  139.4 2.6 %gather.14 = bf16[16,4,16384]{2,1,0:T(4,128)(2,1)S(1)} reshape(bf16[64,128,128]{2,1,0:T(8,128)(2,1)} %gather_fusion) | data formatting | bytes 4194304 | tf_op jit(solution)/shard_map/jit(_take)/gather | solution.py:104
  142.3 1.0 broadcast_select_fusion
  143.3 1.0 pad_maximum_fusion
  144.3 35.0 %all_to_all.9 = bf16[16,4,16385]{2,1,0:T(4,128)(2,1)} all-to-all(bf16[16,4,16385]{2,1,0:T(4,128)(2,1)S(1)} %pad_maximum_fusion), channel_id=1, replica_groups=mesh['rows_0'=4,'rows_1'=4,'cols_0'=4,'cols_1'=2] {'rows_0','rows_1'}, dimensions={0} | all-to-all | bytes 4194560 | tf_op jit(solution)/shard_map/all_to_all | solution.py:25
  179.3 2.8 %all_to_all.7 = bf16[64,16385]{1,0:T(8,128)(2,1)S(1)} reshape(bf16[16,4,16385]{2,1,0:T(4,128)(2,1)} %all_to_all.9) | data formatting | bytes 4194560 | tf_op jit(solution)/shard_map/all_to_all | solution.py:25
  182.1 1.5 slice_bitcast_fusion
  183.9 0.8 scatter_custom_fusion.1
  184.7 2.2 %copy.13 = bf16[8,8,128,128]{3,2,1,0:T(8,128)(2,1)S(1)} copy(bf16[8,8,128,128]{3,1,2,0:T(8,128)(2,1)} %slice_bitcast_fusion) | data formatting | bytes 4194304
  186.9 0.8 gather_fusion.2
  187.6 1.1 broadcast_select_fusion.1
  (55 shorter events, 4.5 us)
Async XLA Ops:
  20.0 25.8 %copy-start.1 = (s32[2,64]{1,0:T(2,128)S(1)}, s32[2,64]{1,0:T(2,128)}, u32[]{:S(2)}) copy-start(s32[2,64]{1,0:T(2,128)} %param.18) | copy-start | bytes 1540
  20.0 25.8 %copy-start.2 = (s32[64]{0:T(128)S(1)}, s32[64]{0:T(128)}, u32[]{:S(2)}) copy-start(s32[64]{0:T(128)} %param.19) | copy-start | bytes 772
  119.4 17.8 %copy-start = (f32[6]{0:T(128)}, f32[6]{0:T(128)S(1)}, u32[]{:S(2)}) copy-start(f32[6]{0:T(128)S(1)} %broadcast_divide_fusion) | copy-start | bytes 76
